TPU v7x, 32 devices: a whole 2x2x4 slice. The times are simulated.
32 devices in a mesh: north: 8 (over y, x, core), deep: 4 (over z).
Axes of the slice: x: 2, y: 2, z: 4, core: 2. Of those that a mesh axis runs over, the one named last changes fastest.
Arguments:
- velocity: float32 [4, 128, 64, 256], P(None, None, 'north', 'deep'), may hold values from -6 to 6
- coupling: float32 [4, 4], replicated, may hold values from -4 to 4
- symbol_x: float32 [128], replicated, may hold values from 0.3 to 3
- symbol_y: float32 [64], replicated, may hold values from 0.3 to 3
- symbol_z: float32 [256], replicated, may hold values from 0.3 to 3
Outputs:
- spectrum: float32 [4, 128, 64, 256], P(None, 'north', 'deep')
All inputs are finite; a program needn't handle non-finite values.
Results may differ from a plain program's by a relative error of at most 0.00007.
Values sent between devices are 32-bit elements; how exact they have to be, the bound alone decides.
A program may use at most 128 MiB of HBM per device.

v0:
```python
import jax
import jax.numpy as jnp
from jax import lax
from jax.sharding import PartitionSpec as P


def basis_table(count):
    rank = jnp.arange(count)
    angle = (
        jnp.pi
        / (count + 1)
        * ((rank[:, None] + 1) * (rank[None, :] + 1) % (2 * count + 2)).astype(jnp.float32)
    )
    return jnp.sin(angle) * (2.0 / (count + 1)) ** 0.5


def along_dim(values, dim):
    moved = jnp.tensordot(
        values, basis_table(values.shape[dim]), axes=([dim], [0]), precision=lax.Precision.HIGHEST
    )
    return jnp.moveaxis(moved, -1, dim)


def on_device(velocity, coupling, symbol_x, symbol_y, symbol_z):
    part_values = velocity
    part_values = along_dim(part_values, 1)
    part_values = lax.all_to_all(part_values, "north", split_axis=1, concat_axis=2, tiled=True)
    part_values = along_dim(part_values, 2)
    block_values = part_values
    block_values = lax.all_to_all(block_values, "deep", split_axis=2, concat_axis=3, tiled=True)
    block_values = along_dim(block_values, 3)
    share_x = block_values.shape[1]
    part_x = lax.dynamic_slice_in_dim(symbol_x, lax.axis_index("north") * share_x, share_x)
    share_y = block_values.shape[2]
    part_y = lax.dynamic_slice_in_dim(symbol_y, lax.axis_index("deep") * share_y, share_y)
    symbol = part_x[:, None, None] + part_y[None, :, None] + symbol_z[None, None, :]
    weight_xyz = 1.0 / (1.0 + symbol)
    mixed_fields = jnp.einsum(
        "ab,bxyz->axyz", coupling, block_values, precision=lax.Precision.HIGHEST
    )
    block_values = weight_xyz * block_values + (1.0 - weight_xyz) * mixed_fields
    return block_values


def solution(mesh):
    placed = (P(None, None, "north", "deep"), P(), P(), P(), P())
    return jax.shard_map(
        on_device,
        mesh=mesh,
        in_specs=placed,
        out_specs=P(None, "north", "deep", None),
        check_vma=False,
    )
```

profile of v0, /device:TPU:2, one launch (start us, length us, event | category | flops | bytes accessed | tf_op | source)
XLA Modules:
  0.0 93.1 jit_solution(7834806281157115720)
XLA Ops:
  0.0 1.2 %copy-done = f32[4,128,8,64]{1,3,2,0:T(8,128)S(1)} copy-done((f32[4,128,8,64]{1,3,2,0:T(8,128)S(1)}, f32[4,128,8,64]{1,3,2,0:T(8,128)}, u32[]{:S(2)}) %copy-start) | copy-done | bytes 1048600
  1.2 2.3 %fusion.29 = f32[128,2048]{0,1} fusion(f32[128,2048]{0,1:T(8,128)S(1)} %bitcast.42, s32[128]{0:T(128)S(1)} %iota_add_fusion.2), kind=kOutput, calls=%fused_computation.32 | convolution fusion | flops 402817024 | bytes 2097664
  3.5 3.1 %copy.17 = f32[4,128,8,64]{3,2,0,1:T(8,128)S(1)} copy(f32[4,128,8,64]{1,3,2,0:T(8,128)} %bitcast.47) | data formatting | bytes 2097152 | tf_op jit(solution)/shard_map/transpose | solution.py:21
  6.6 2.1 %reshape.72 = f32[8,1,32768]{2,1,0:T(1,128)} reshape(f32[128,4,8,64]{3,2,1,0:T(8,128)S(1)} %bitcast.44) | data formatting | bytes 2097152
  8.7 4.3 %all-to-all-start = ((f32[8,1,32768]{2,1,0:T(1,128)}), f32[8,1,32768]{2,1,0:T(1,128)S(1)}, u32[]{:S(2)}, u32[]{:S(2)}) async-start(f32[8,1,32768]{2,1,0:T(1,128)} %reshape.72), calls=%async_computation | async-start | bytes 2097152 | tf_op jit(solution)/shard_map/all_to_all | solution.py:27
  12.9 13.9 %all-to-all-done = f32[8,1,32768]{2,1,0:T(1,128)S(1)} async-done(((f32[8,1,32768]{2,1,0:T(1,128)}), f32[8,1,32768]{2,1,0:T(1,128)S(1)}, u32[]{:S(2)}, u32[]{:S(2)}) %all-to-all-start) | async-done | bytes 1048608 | tf_op jit(solution)/shard_map/all_to_all | solution.py:27
  26.8 0.6 broadcast.101
  27.4 4.5 %reduce = f32[8,32768]{1,0:T(8,128)} reduce(f32[8,1,32768]{2,1,0:T(1,128)S(1)} %all-to-all-done, f32[]{:T(128)} %broadcast.101), dimensions={1}, to_apply=%all_to_all.26.reduce_sub_computation | reduce | bytes 2097156 | tf_op jit(solution)/shard_map/all_to_all | solution.py:27
  31.9 2.1 %reshape.73 = f32[128,4,8,64]{3,2,1,0:T(8,128)S(1)} reshape(f32[8,32768]{1,0:T(8,128)} %reduce) | data formatting | bytes 2097152
  33.9 4.8 %fusion.3 = f32[4,16,64,64]{2,3,1,0:T(8,128)} fusion(f32[4,16,8,8,64]{4,3,0,1,2:T(8,128)S(1)} %bitcast.43, s32[64]{0:T(128)S(1)} %iota_add_fusion.1), kind=kOutput, calls=%fused_computation.3 | convolution fusion | flops 201367552 | bytes 2097408 | tf_op jit(solution)/shard_map/dot_general | solution.py:18
  38.7 3.1 %copy.21 = f32[4,16,64,64]{3,1,0,2:T(8,128)S(1)} copy(f32[4,16,64,64]{2,3,1,0:T(8,128)} %fusion.3) | data formatting | bytes 2097152 | tf_op jit(solution)/shard_map/transpose | solution.py:21
  41.9 2.4 %reshape.74 = f32[4,1,65536]{2,1,0:T(1,128)} reshape(f32[64,4,16,64]{3,2,1,0:T(8,128)S(1)} %bitcast.45) | data formatting | bytes 2097152
  44.3 4.9 %all-to-all-start.1 = ((f32[4,1,65536]{2,1,0:T(1,128)}), f32[4,1,65536]{2,1,0:T(1,128)S(1)}, u32[]{:S(2)}, u32[]{:S(2)}) async-start(f32[4,1,65536]{2,1,0:T(1,128)} %reshape.74), calls=%async_computation.1 | async-start | bytes 2097152 | tf_op jit(solution)/shard_map/all_to_all | solution.py:30
  49.2 0.1 dynamic_slice.7
  49.2 0.1 dynamic_slice.6
  49.4 0.8 add_divide_fusion
  50.2 24.9 %all-to-all-done.1 = f32[4,1,65536]{2,1,0:T(1,128)S(1)} async-done(((f32[4,1,65536]{2,1,0:T(1,128)}), f32[4,1,65536]{2,1,0:T(1,128)S(1)}, u32[]{:S(2)}, u32[]{:S(2)}) %all-to-all-start.1) | async-done | bytes 1048608 | tf_op jit(solution)/shard_map/all_to_all | solution.py:30
  75.1 4.6 %reduce.1 = f32[4,65536]{1,0:T(4,128)} reduce(f32[4,1,65536]{2,1,0:T(1,128)S(1)} %all-to-all-done.1, f32[]{:T(128)} %broadcast.101), dimensions={1}, to_apply=%all_to_all.30.reduce_sub_computation | reduce | bytes 2097156 | tf_op jit(solution)/shard_map/all_to_all | solution.py:30
  79.7 2.2 %reshape.75 = f32[64,4,16,64]{3,2,1,0:T(8,128)S(1)} reshape(f32[4,65536]{1,0:T(4,128)} %reduce.1) | data formatting | bytes 2097152
  82.0 2.7 %copy.23 = f32[4,16,16,4,64]{4,3,2,1,0:T(4,128)} copy(f32[4,16,16,4,64]{4,1,0,2,3:T(8,128)S(1)} %bitcast.46) | data formatting | bytes 2097152 | tf_op jit(solution)/shard_map/all_to_all | solution.py:30
  84.7 2.5 %all_to_all.33 = f32[4,16,16,256]{3,2,1,0:T(8,128)S(1)} reshape(f32[4,16,16,4,64]{4,3,2,1,0:T(4,128)} %copy.23) | data formatting | bytes 2097152 | tf_op jit(solution)/shard_map/all_to_all | solution.py:30
  87.2 2.1 %fusion.13 = f32[4,16,16,256]{3,2,1,0:T(8,128)S(1)} fusion(f32[4,16,16,256]{3,2,1,0:T(8,128)S(1)} %all_to_all.33, s32[256]{0:T(256)S(1)} %iota_add_fusion), kind=kOutput, calls=%fused_computation.14 | convolution fusion | flops 805961728 | bytes 2098176 | tf_op jit(solution)/shard_map/dot_general | solution.py:18
  89.3 2.5 %fusion.6 = f32[16,16,256,4]{2,3,1,0:T(4,128)S(1)} fusion(f32[4,16,16,256]{3,2,1,0:T(8,128)S(1)} %fusion.13, f32[4,4]{1,0:T(4,128)S(1)} %copy-done.2), kind=kOutput, calls=%fused_computation.6 | convolution fusion | flops 12582912 | bytes 2097216 | tf_op jit(solution)/shard_map/ab,bxyz->axyz/dot_general | solution.py:38
  91.8 1.3 %bitcast_add_fusion = f32[4,16,16,256]{3,2,1,0:T(8,128)} fusion(f32[16,16,256,4]{2,3,1,0:T(4,128)S(1)} %fusion.6, f32[4,16,16,256]{3,2,1,0:T(8,128)S(1)} %fusion.13, f32[16,16,256]{2,1,0:T(8,128)S(1)} %copy-done.1, f32[16,16,256]{2,1,0:T(8,128)S(1)} %get-tuple-element.5), kind=kLoop, calls=%fused_computation.4 | loop fusion | flops 786432 | bytes 3670016 | tf_op jit(solution)/shard_map/add | solution.py:41
  (15 shorter events, 0.1 us)
Async XLA Ops:
  0.0 1.2 %copy-start = (f32[4,128,8,64]{1,3,2,0:T(8,128)S(1)}, f32[4,128,8,64]{1,3,2,0:T(8,128)}, u32[]{:S(2)}) copy-start(f32[4,128,8,64]{1,3,2,0:T(8,128)} %param.5) | copy-start | bytes 3145732
  8.7 18.1 %all-to-all-start = ((f32[8,1,32768]{2,1,0:T(1,128)}), f32[8,1,32768]{2,1,0:T(1,128)S(1)}, u32[]{:S(2)}, u32[]{:S(2)}) async-start(f32[8,1,32768]{2,1,0:T(1,128)} %reshape.72), calls=%async_computation | async-start | bytes 2097152 | tf_op jit(solution)/shard_map/all_to_all | solution.py:27
  41.9 7.3 %copy-start.4 = (f32[64]{0:T(128)S(1)}, f32[64]{0:T(128)}, u32[]{:S(2)}) copy-start(f32[64]{0:T(128)} %param.8) | copy-start | bytes 772
  41.9 7.4 %copy-start.5 = (f32[128]{0:T(128)S(1)}, f32[128]{0:T(128)}, u32[]{:S(2)}) copy-start(f32[128]{0:T(128)} %param.7) | copy-start | bytes 1540
  41.9 7.5 %copy-start.3 = (f32[256]{0:T(256)S(1)}, f32[256]{0:T(256)}, u32[]{:S(2)}) copy-start(f32[256]{0:T(256)} %param.9) | copy-start | bytes 3076
  44.3 30.8 %all-to-all-start.1 = ((f32[4,1,65536]{2,1,0:T(1,128)}), f32[4,1,65536]{2,1,0:T(1,128)S(1)}, u32[]{:S(2)}, u32[]{:S(2)}) async-start(f32[4,1,65536]{2,1,0:T(1,128)} %reshape.74), calls=%async_computation.1 | async-start | bytes 2097152 | tf_op jit(solution)/shard_map/all_to_all | solution.py:30
  84.7 4.6 %copy-start.2 = (f32[4,4]{1,0:T(4,128)S(1)}, f32[4,4]{1,0:T(4,128)}, u32[]{:S(2)}) copy-start(f32[4,4]{1,0:T(4,128)} %param.6) | copy-start | bytes 196
  87.2 4.6 %copy-start.1 = (f32[16,16,256]{2,1,0:T(8,128)S(1)}, f32[16,16,256]{2,1,0:T(8,128)}, u32[]{:S(2)}) copy-start(f32[16,16,256]{2,1,0:T(8,128)} %get-tuple-element.6) | copy-start | bytes 786436
where the time goes:
time: 93.5 us; the launch traced here: 93.1 us
  waiting for transfers between devices  38.8 us (41%)
  local copies, waits for them, and re-layouts  22.1 us (24%)
  matrix products  11.6 us (12%)
  other arithmetic  11.3 us (12%)
  starting transfers between devices  9.12 us (10%)
    all_to_all x1, waiting for transfers between devices, on_device(): lax.all_to_all(block_values, 'deep', split_axis=2, concat_axis=3, tiled=T...  24.9 us
    all_to_all x1, waiting for transfers between devices, on_device(): lax.all_to_all(part_values, 'north', split_axis=1, concat_axis=2, tiled=T...  13.9 us
    unnamed x16, local copies, waits for them, and re-layouts  10.1 us
    dot_general x2, matrix products, along_dim(): jnp.tensordot(values, basis_table(values.shape[dim]), axes=([dim], [0]),...  6.89 us
    transpose x2, local copies, waits for them, and re-layouts, along_dim(): return jnp.moveaxis(moved, -1, dim)  6.15 us
    all_to_all x2, local copies, waits for them, and re-layouts, on_device(): lax.all_to_all(block_values, 'deep', split_axis=2, concat_axis=3, tiled=T...  5.19 us
    all_to_all x1, starting transfers between devices, on_device(): lax.all_to_all(block_values, 'deep', split_axis=2, concat_axis=3, tiled=T...  4.87 us
    all_to_all x1, other arithmetic, on_device(): lax.all_to_all(block_values, 'deep', split_axis=2, concat_axis=3, tiled=T...  4.63 us
  transfers between devices with their start and end apart: 2, of which 2 were waited for; matrix products, arithmetic and copies ran while one was open for 1% of the time, Pallas kernels for 0%

commit v1 on v0

v1 whole, which is shorter than its diff:
```python
import functools

import jax
import jax.numpy as jnp
import numpy as np
from jax import lax
from jax.experimental import pallas as pl
from jax.experimental.pallas import tpu as pltpu
from jax.sharding import PartitionSpec as P

LANES = 128
CHUNKS = 8
F32 = jnp.float32
BF16 = jnp.bfloat16
MESH = pl.DeviceIdType.MESH


def basis_table(count):
    rank = np.arange(1, count + 1)
    turns = (rank[:, None] * rank[None, :]) % (2 * count + 2)
    table = np.sin(np.pi / (count + 1) * turns) * (2.0 / (count + 1)) ** 0.5
    table = table.astype(np.float32)
    high = table.astype(jnp.bfloat16)
    low = (table - high.astype(np.float32)).astype(jnp.bfloat16)
    return high, low


def split(values):
    high = values.astype(BF16)
    low = (values - high.astype(F32)).astype(BF16)
    return high, low


def kernel(
    north, deep, chunks,
    a_hbm, coupling, sym_x, sym_y, sym_z, tx_hbm, ty_hbm, tz_hbm,
    out,
    a, tx, ty, tz, x1, r, s, t,
    load_sem, send_n, recv_n, send_d, recv_d,
):
    me_n = lax.axis_index("north")
    me_d = lax.axis_index("deep")
    fields, share_y, share_z, size_x = a.shape
    pack = LANES // share_z
    packs = fields // pack
    share_x = size_x // north
    size_y = share_y * north
    block_y = size_y // deep
    size_z = share_z * deep
    step = share_x // chunks
    half = deep // 2

    loads = [pltpu.make_async_copy(tx_hbm, tx, load_sem.at[0])]
    for p in range(packs):
        part = pl.ds(p * pack, pack)
        loads.append(pltpu.make_async_copy(a_hbm.at[part], a.at[part], load_sem.at[1 + p]))
    late = [
        pltpu.make_async_copy(ty_hbm, ty, load_sem.at[1 + packs]),
        pltpu.make_async_copy(tz_hbm, tz, load_sem.at[2 + packs]),
    ]
    for copy in loads + late:
        copy.start()

    peers_n = [lax.rem(me_n + k, north) for k in range(1, north)]
    side = me_d // half
    peers_d = [(1 - side) * half + lax.rem(me_d + j, half) for j in range(half)]
    peers_d += [side * half + lax.rem(me_d + j, half) for j in range(1, half)]

    barrier = pltpu.get_barrier_semaphore()
    for peer in peers_n:
        pl.semaphore_signal(barrier, inc=1, device_id={"north": peer}, device_id_type=MESH)
    for peer in peers_d:
        pl.semaphore_signal(barrier, inc=1, device_id={"deep": peer}, device_id_type=MESH)

    loads[0].wait()
    for p in range(packs):
        loads[1 + p].wait()
        for y in range(share_y):
            rows = jnp.concatenate([a[p * pack + f, y] for f in range(pack)], axis=0)
            high, low = split(rows)
            dot = functools.partial(
                lax.dot_general,
                dimension_numbers=(((1,), (1,)), ((), ())),
                preferred_element_type=F32,
            )
            x1[p, :, y, :] = dot(tx[0], high) + dot(tx[1], high) + dot(tx[0], low)

    pl.semaphore_wait(barrier, len(peers_n) + len(peers_d))

    def north_copy(c, peer, slot):
        return pltpu.make_async_remote_copy(
            src_ref=x1.at[:, pl.ds(peer * share_x + c * step, step)],
            dst_ref=r.at[:, pl.ds(c * step, step), pl.ds(pl.multiple_of(me_n * share_y, 8), share_y)],
            send_sem=send_n.at[c, slot],
            recv_sem=recv_n.at[c, slot],
            device_id={"north": peer},
            device_id_type=MESH,
        )

    def deep_copy(c, peer, source):
        return pltpu.make_async_remote_copy(
            src_ref=s.at[:, pl.ds(c * step, step), pl.ds(pl.multiple_of(peer * block_y, 8), block_y)],
            dst_ref=t.at[me_d, :, pl.ds(c * step, step)],
            send_sem=send_d.at[c, peer],
            recv_sem=recv_d.at[c, source],
            device_id={"deep": peer},
            device_id_type=MESH,
        )

    for c in range(chunks):
        for slot, peer in enumerate(peers_n):
            north_copy(c, peer, slot).start()

    own_rows = pl.ds(pl.multiple_of(me_n * share_y, 8), share_y)
    r[:, :, own_rows, :] = x1[:, pl.ds(me_n * share_x, share_x)]

    rows_y = lax.broadcasted_iota(jnp.int32, (block_y, size_z), 0)
    base = jnp.broadcast_to(sym_z[...], (block_y, size_z))
    column = jnp.zeros((block_y, size_z), F32)
    for i in range(block_y):
        column = jnp.where(rows_y == i, sym_y[me_d * block_y + i], column)
    base = base + column

    for copy in late:
        copy.wait()

    for c in range(chunks):
        for slot, peer in enumerate(peers_n):
            north_copy(c, peer, slot).wait_recv()
        for p in range(packs):
            for x in range(c * step, (c + 1) * step, 2):
                width = min(2, (c + 1) * step - x)
                high, low = split(jnp.concatenate([r[p, x + i] for i in range(width)], axis=1))
                stack = jnp.concatenate([high, high, low], axis=0)
                mixed = jnp.dot(ty[...], stack, preferred_element_type=F32)
                for i in range(width):
                    s[p, x + i] = mixed[:, i * LANES:(i + 1) * LANES]
        for peer in peers_d:
            deep_copy(c, peer, me_d).start()

    own_block = pl.ds(pl.multiple_of(me_d * block_y, 8), block_y)
    t[me_d] = s[:, :, own_block, :]

    for c in range(chunks):
        for peer in peers_d:
            deep_copy(c, peer, peer).wait_recv()
        spectrum = []
        for p in range(packs):
            parts = [
                t[d, p, c * step:(c + 1) * step].reshape(step * block_y, LANES)
                for d in range(deep)
            ]
            for f in range(pack):
                rows = jnp.concatenate(
                    [part[:, f * share_z:(f + 1) * share_z] for part in parts], axis=1
                )
                high, low = split(rows)
                spectrum.append(
                    jnp.dot(high, tz[0], preferred_element_type=F32)
                    + jnp.dot(high, tz[1], preferred_element_type=F32)
                    + jnp.dot(low, tz[0], preferred_element_type=F32)
                )
        for i in range(step):
            x = c * step + i
            weight = 1.0 / (1.0 + (base + sym_x[me_n * share_x + x]))
            rest = 1.0 - weight
            old = [value[i * block_y:(i + 1) * block_y] for value in spectrum]
            for f in range(fields):
                total = coupling[f, 0] * old[0]
                for g in range(1, fields):
                    total = total + coupling[f, g] * old[g]
                out[f, x] = weight * old[f] + rest * total

    for c in range(chunks):
        for slot, peer in enumerate(peers_n):
            north_copy(c, peer, slot).wait_send()
        for peer in peers_d:
            deep_copy(c, peer, me_d).wait_send()


def on_device(north, deep, velocity, coupling, symbol_x, symbol_y, symbol_z):
    field = jnp.transpose(velocity, (0, 2, 3, 1))
    fields, share_y, share_z, size_x = field.shape
    size_y, size_z = share_y * north, share_z * deep
    share_x, block_y = size_x // north, size_y // deep
    packs = fields * share_z // LANES
    chunks = min(CHUNKS, share_x)
    high, low = basis_table(size_x)
    tx = jnp.asarray(np.stack([high, low]))
    high, low = basis_table(size_y)
    ty = jnp.asarray(np.concatenate([high, low, high], axis=1))
    high, low = basis_table(size_z)
    tz = jnp.asarray(np.stack([high, low]))
    smem = pl.BlockSpec(memory_space=pltpu.SMEM)
    vmem = pl.BlockSpec(memory_space=pltpu.VMEM)
    hbm = pl.BlockSpec(memory_space=pl.ANY)
    return pl.pallas_call(
        functools.partial(kernel, north, deep, chunks),
        out_shape=jax.ShapeDtypeStruct((fields, share_x, block_y, size_z), F32),
        in_specs=[hbm, smem, smem, smem, vmem, hbm, hbm, hbm],
        out_specs=vmem,
        scratch_shapes=[
            pltpu.VMEM(field.shape, F32),
            pltpu.VMEM(tx.shape, BF16),
            pltpu.VMEM(ty.shape, BF16),
            pltpu.VMEM(tz.shape, BF16),
            pltpu.VMEM((packs, size_x, share_y, LANES), F32),
            pltpu.VMEM((packs, share_x, size_y, LANES), F32),
            pltpu.VMEM((packs, share_x, size_y, LANES), F32),
            pltpu.VMEM((deep, packs, share_x, block_y, LANES), F32),
            pltpu.SemaphoreType.DMA((3 + packs,)),
            pltpu.SemaphoreType.DMA((chunks, north - 1)),
            pltpu.SemaphoreType.DMA((chunks, north - 1)),
            pltpu.SemaphoreType.DMA((chunks, deep)),
            pltpu.SemaphoreType.DMA((chunks, deep)),
        ],
        compiler_params=pltpu.CompilerParams(collective_id=0, has_side_effects=True),
    )(field, coupling, symbol_x, symbol_y, symbol_z[None, :], tx, ty, tz)


def solution(mesh):
    placed = (P(None, None, "north", "deep"), P(), P(), P(), P())
    return jax.shard_map(
        functools.partial(on_device, mesh.shape["north"], mesh.shape["deep"]),
        mesh=mesh,
        in_specs=placed,
        out_specs=P(None, "north", "deep", None),
        check_vma=False,
    )
```

time: 93.5 us -> 40.8 us (0.44)
  the two profiles are of different devices: /device:TPU:2 before, /device:TPU:1 now
where the time goes in v1:
time: 40.8 us; the launch traced here: 40 us
  Pallas kernels  37.7 us (92%)
  local copies, waits for them, and re-layouts  2.26 us (6%)
    pallas_call x1, Pallas kernels, on_device(): pl.pallas_call(functools.partial(kernel, north, deep, chunks), out_shape=...  37.7 us
    unnamed x1, local copies, waits for them, and re-layouts  2.26 us

profile of v1, /device:TPU:1, one launch (start us, length us, event | category | flops | bytes accessed | tf_op | source)
XLA Modules:
  0.0 40.0 jit_solution(4452890810221487553)
XLA Ops:
  0.0 37.7 %shard_map.82 = f32[4,16,16,256]{3,2,1,0:T(8,128)} custom-call(f32[4,8,64,128]{3,2,1,0:T(8,128)} %bitcast.2, f32[4,4]{1,0:T(4,128)} %coupling.1, f32[128]{0:T(128)} %sym_x.1, f32[64]{0:T(128)} %sym_y.1, f32[1,256]{1,0:T(1,128)} %bitcast.3, bf16[2,128,128]{2,1,0:T(8,128)(2,1)} %constant.6.clone.tx_hbm, bf16[64,192]{1,0:T(8,128)(2,1)} %constant.7.clone.ty_hbm, ...), custom_call_target="tpu_custom_call" | custom-call | tf_op jit(solution)/shard_map/pallas_call | solution.py:197
  37.7 2.3 %copy.10 = f32[4,16,16,256]{3,2,1,0:T(8,128)} copy(f32[4,16,16,256]{3,2,1,0:T(8,128)} %shard_map.82) | data formatting | bytes 2097152

commit v2 on v1

--- a/solution.py
+++ b/solution.py
@@ -33,9 +33,9 @@
 
 def kernel(
     north, deep, chunks,
-    a_hbm, coupling, sym_x, sym_y, sym_z, tx_hbm, ty_hbm, tz_hbm,
+    a_hbm, coupling_hbm, sym_x_hbm, sym_y_hbm, sym_z_hbm, tx_hbm, ty_hbm, tz_hbm,
     out,
-    a, tx, ty, tz, x1, r, s, t,
+    a, coupling, sym_x, sym_y, sym_z, tx, ty, tz, x1, r, s, t,
     load_sem, send_n, recv_n, send_d, recv_d,
 ):
     me_n = lax.axis_index("north")
@@ -54,9 +54,13 @@
     for p in range(packs):
         part = pl.ds(p * pack, pack)
         loads.append(pltpu.make_async_copy(a_hbm.at[part], a.at[part], load_sem.at[1 + p]))
+    pairs = [
+        (ty_hbm, ty), (sym_x_hbm, sym_x), (sym_y_hbm, sym_y), (sym_z_hbm, sym_z),
+        (coupling_hbm, coupling), (tz_hbm, tz),
+    ]
     late = [
-        pltpu.make_async_copy(ty_hbm, ty, load_sem.at[1 + packs]),
-        pltpu.make_async_copy(tz_hbm, tz, load_sem.at[2 + packs]),
+        pltpu.make_async_copy(source, target, load_sem.at[1 + packs + i])
+        for i, (source, target) in enumerate(pairs)
     ]
     for copy in loads + late:
         copy.start()
@@ -75,15 +79,17 @@
     loads[0].wait()
     for p in range(packs):
         loads[1 + p].wait()
-        for y in range(share_y):
-            rows = jnp.concatenate([a[p * pack + f, y] for f in range(pack)], axis=0)
-            high, low = split(rows)
-            dot = functools.partial(
-                lax.dot_general,
+        for y in range(0, share_y, 2):
+            rows = [a[p * pack + f, y + i] for i in range(2) for f in range(pack)]
+            high, low = split(jnp.concatenate(rows, axis=0))
+            lines = lax.dot_general(
+                tx[...],
+                jnp.concatenate([high, high, low], axis=1),
                 dimension_numbers=(((1,), (1,)), ((), ())),
                 preferred_element_type=F32,
             )
-            x1[p, :, y, :] = dot(tx[0], high) + dot(tx[1], high) + dot(tx[0], low)
+            x1[p, :, y, :] = lines[:, :LANES]
+            x1[p, :, y + 1, :] = lines[:, LANES:]
 
     pl.semaphore_wait(barrier, len(peers_n) + len(peers_d))
 
@@ -114,15 +120,15 @@
     own_rows = pl.ds(pl.multiple_of(me_n * share_y, 8), share_y)
     r[:, :, own_rows, :] = x1[:, pl.ds(me_n * share_x, share_x)]
 
+    for copy in late:
+        copy.wait()
+
     rows_y = lax.broadcasted_iota(jnp.int32, (block_y, size_z), 0)
     base = jnp.broadcast_to(sym_z[...], (block_y, size_z))
     column = jnp.zeros((block_y, size_z), F32)
     for i in range(block_y):
-        column = jnp.where(rows_y == i, sym_y[me_d * block_y + i], column)
+        column = jnp.where(rows_y == i, sym_y[0, me_d * block_y + i], column)
     base = base + column
-
-    for copy in late:
-        copy.wait()
 
     for c in range(chunks):
         for slot, peer in enumerate(peers_n):
@@ -162,7 +168,7 @@
                 )
         for i in range(step):
             x = c * step + i
-            weight = 1.0 / (1.0 + (base + sym_x[me_n * share_x + x]))
+            weight = 1.0 / (1.0 + (base + sym_x[0, me_n * share_x + x]))
             rest = 1.0 - weight
             old = [value[i * block_y:(i + 1) * block_y] for value in spectrum]
             for f in range(fields):
@@ -186,21 +192,26 @@
     packs = fields * share_z // LANES
     chunks = min(CHUNKS, share_x)
     high, low = basis_table(size_x)
-    tx = jnp.asarray(np.stack([high, low]))
+    tx = jnp.asarray(np.concatenate([high, low, high], axis=1))
     high, low = basis_table(size_y)
     ty = jnp.asarray(np.concatenate([high, low, high], axis=1))
     high, low = basis_table(size_z)
     tz = jnp.asarray(np.stack([high, low]))
-    smem = pl.BlockSpec(memory_space=pltpu.SMEM)
+    need = 4 * field.size * 7 + 2 * (tx.size + ty.size + tz.size) + 2**21
     vmem = pl.BlockSpec(memory_space=pltpu.VMEM)
-    hbm = pl.BlockSpec(memory_space=pl.ANY)
+    hbm = pl.BlockSpec(memory_space=pltpu.HBM)
+    operands = (field, coupling, symbol_x[None, :], symbol_y[None, :], symbol_z[None, :], tx, ty, tz)
     return pl.pallas_call(
         functools.partial(kernel, north, deep, chunks),
         out_shape=jax.ShapeDtypeStruct((fields, share_x, block_y, size_z), F32),
-        in_specs=[hbm, smem, smem, smem, vmem, hbm, hbm, hbm],
+        in_specs=[hbm] * 8,
         out_specs=vmem,
         scratch_shapes=[
             pltpu.VMEM(field.shape, F32),
+            pltpu.SMEM(coupling.shape, F32),
+            pltpu.SMEM((1, size_x), F32),
+            pltpu.SMEM((1, size_y), F32),
+            pltpu.VMEM((1, size_z), F32),
             pltpu.VMEM(tx.shape, BF16),
             pltpu.VMEM(ty.shape, BF16),
             pltpu.VMEM(tz.shape, BF16),
@@ -208,14 +219,16 @@
             pltpu.VMEM((packs, share_x, size_y, LANES), F32),
             pltpu.VMEM((packs, share_x, size_y, LANES), F32),
             pltpu.VMEM((deep, packs, share_x, block_y, LANES), F32),
-            pltpu.SemaphoreType.DMA((3 + packs,)),
+            pltpu.SemaphoreType.DMA((7 + packs,)),
             pltpu.SemaphoreType.DMA((chunks, north - 1)),
             pltpu.SemaphoreType.DMA((chunks, north - 1)),
             pltpu.SemaphoreType.DMA((chunks, deep)),
             pltpu.SemaphoreType.DMA((chunks, deep)),
         ],
-        compiler_params=pltpu.CompilerParams(collective_id=0, has_side_effects=True),
-    )(field, coupling, symbol_x, symbol_y, symbol_z[None, :], tx, ty, tz)
+        compiler_params=pltpu.CompilerParams(
+            collective_id=0, has_side_effects=True, vmem_limit_bytes=need
+        ),
+    )(*[pltpu.with_memory_space_constraint(v, pltpu.HBM) for v in operands])
 
 
 def solution(mesh):

time: 40.8 us -> 37.4 us (0.917)
  Pallas kernels: 37.7 us -> 35.7 us
  local copies, waits for them, and re-layouts: 2.26 us -> 0.97 us
    pallas_call x1, Pallas kernels: 37.7 us -> 35.7 us  [on_device(): pl.pallas_call(functools.partial(kernel, north, deep, chunks), out_shape=...]
    unnamed x1, local copies, waits for them, and re-layouts: 2.26 us -> 0.97 us
where the time goes in v2:
time: 37.4 us; the launch traced here: 36.7 us
  Pallas kernels  35.7 us (95%)
  local copies, waits for them, and re-layouts  0.97 us (3%)
    pallas_call x1, Pallas kernels, on_device(): pl.pallas_call(functools.partial(kernel, north, deep, chunks), out_shape=...  35.7 us
    unnamed x1, local copies, waits for them, and re-layouts  0.97 us

profile of v2, /device:TPU:1, one launch (start us, length us, event | category | flops | bytes accessed | tf_op | source)
XLA Modules:
  0.0 36.7 jit_solution(18180618925926205963)
XLA Ops:
  0.0 35.7 %shard_map.82 = f32[4,16,16,256]{3,2,1,0:T(8,128)S(1)} custom-call(f32[4,8,64,128]{3,2,1,0:T(8,128)} %bitcast.4, f32[4,4]{1,0:T(4,128)} %coupling_hbm.1, f32[1,128]{1,0:T(1,128)} %bitcast.6, f32[1,64]{1,0:T(1,128)} %bitcast.7, f32[1,256]{1,0:T(1,128)} %bitcast.5, bf16[128,384]{1,0:T(8,128)(2,1)} %constant.6.clone.tx_hbm, ...), custom_call_target="tpu_custom_call" | custom-call | tf_op jit(solution)/shard_map/pallas_call | solution.py:204
  35.7 1.0 %copy.10 = f32[4,16,16,256]{3,2,1,0:T(8,128)} copy(f32[4,16,16,256]{3,2,1,0:T(8,128)S(1)} %shard_map.82) | data formatting | bytes 2097152

commit v3 on v2

--- a/solution.py
+++ b/solution.py
@@ -9,7 +9,7 @@
 from jax.sharding import PartitionSpec as P
 
 LANES = 128
-CHUNKS = 8
+SIZES = (3, 5, 8)
 F32 = jnp.float32
 BF16 = jnp.bfloat16
 MESH = pl.DeviceIdType.MESH
@@ -47,7 +47,9 @@
     size_y = share_y * north
     block_y = size_y // deep
     size_z = share_z * deep
-    step = share_x // chunks
+    starts = [sum(chunks[:c]) for c in range(len(chunks))]
+    pieces = [(p, 1, starts[0], chunks[0]) for p in range(packs)]
+    pieces += [(0, packs, starts[c], chunks[c]) for c in range(1, len(chunks))]
     half = deep // 2
 
     loads = [pltpu.make_async_copy(tx_hbm, tx, load_sem.at[0])]
@@ -76,6 +78,28 @@
     for peer in peers_d:
         pl.semaphore_signal(barrier, inc=1, device_id={"deep": peer}, device_id_type=MESH)
 
+    def north_copy(c, peer, slot):
+        p, count, x, size = pieces[c]
+        return pltpu.make_async_remote_copy(
+            src_ref=x1.at[pl.ds(peer * share_x + x, size), pl.ds(p, count)],
+            dst_ref=r.at[me_n, pl.ds(x, size), pl.ds(p, count)],
+            send_sem=send_n.at[c, slot],
+            recv_sem=recv_n.at[c, slot],
+            device_id={"north": peer},
+            device_id_type=MESH,
+        )
+
+    def deep_copy(c, peer, source):
+        p, count, x, size = pieces[c]
+        return pltpu.make_async_remote_copy(
+            src_ref=s.at[peer, pl.ds(x, size), pl.ds(p, count)],
+            dst_ref=t.at[me_d, pl.ds(x, size), pl.ds(p, count)],
+            send_sem=send_d.at[c, peer],
+            recv_sem=recv_d.at[c, source],
+            device_id={"deep": peer},
+            device_id_type=MESH,
+        )
+
     loads[0].wait()
     for p in range(packs):
         loads[1 + p].wait()
@@ -88,37 +112,18 @@
                 dimension_numbers=(((1,), (1,)), ((), ())),
                 preferred_element_type=F32,
             )
-            x1[p, :, y, :] = lines[:, :LANES]
-            x1[p, :, y + 1, :] = lines[:, LANES:]
-
-    pl.semaphore_wait(barrier, len(peers_n) + len(peers_d))
-
-    def north_copy(c, peer, slot):
-        return pltpu.make_async_remote_copy(
-            src_ref=x1.at[:, pl.ds(peer * share_x + c * step, step)],
-            dst_ref=r.at[:, pl.ds(c * step, step), pl.ds(pl.multiple_of(me_n * share_y, 8), share_y)],
-            send_sem=send_n.at[c, slot],
-            recv_sem=recv_n.at[c, slot],
-            device_id={"north": peer},
-            device_id_type=MESH,
-        )
-
-    def deep_copy(c, peer, source):
-        return pltpu.make_async_remote_copy(
-            src_ref=s.at[:, pl.ds(c * step, step), pl.ds(pl.multiple_of(peer * block_y, 8), block_y)],
-            dst_ref=t.at[me_d, :, pl.ds(c * step, step)],
-            send_sem=send_d.at[c, peer],
-            recv_sem=recv_d.at[c, source],
-            device_id={"deep": peer},
-            device_id_type=MESH,
-        )
-
-    for c in range(chunks):
+            x1[:, p, y, :] = lines[:, :LANES]
+            x1[:, p, y + 1, :] = lines[:, LANES:]
+        if p == 0:
+            pl.semaphore_wait(barrier, len(peers_n) + len(peers_d))
+        for slot, peer in enumerate(peers_n):
+            north_copy(p, peer, slot).start()
+
+    for c in range(packs, len(pieces)):
         for slot, peer in enumerate(peers_n):
             north_copy(c, peer, slot).start()
 
-    own_rows = pl.ds(pl.multiple_of(me_n * share_y, 8), share_y)
-    r[:, :, own_rows, :] = x1[:, pl.ds(me_n * share_x, share_x)]
+    r[me_n] = x1[pl.ds(me_n * share_x, share_x)]
 
     for copy in late:
         copy.wait()
@@ -130,30 +135,37 @@
         column = jnp.where(rows_y == i, sym_y[0, me_d * block_y + i], column)
     base = base + column
 
-    for c in range(chunks):
+    for c in range(len(pieces)):
+        first, count, start, size = pieces[c]
         for slot, peer in enumerate(peers_n):
             north_copy(c, peer, slot).wait_recv()
-        for p in range(packs):
-            for x in range(c * step, (c + 1) * step, 2):
-                width = min(2, (c + 1) * step - x)
-                high, low = split(jnp.concatenate([r[p, x + i] for i in range(width)], axis=1))
+        for p in range(first, first + count):
+            for x in range(start, start + size, 2):
+                width = min(2, start + size - x)
+                lines = [
+                    jnp.concatenate([r[n, x + i, p] for n in range(north)], axis=0)
+                    for i in range(width)
+                ]
+                high, low = split(jnp.concatenate(lines, axis=1))
                 stack = jnp.concatenate([high, high, low], axis=0)
                 mixed = jnp.dot(ty[...], stack, preferred_element_type=F32)
                 for i in range(width):
-                    s[p, x + i] = mixed[:, i * LANES:(i + 1) * LANES]
+                    modes = mixed[:, i * LANES:(i + 1) * LANES]
+                    for d in range(deep):
+                        s[d, x + i, p] = modes[d * block_y:(d + 1) * block_y]
         for peer in peers_d:
             deep_copy(c, peer, me_d).start()
 
-    own_block = pl.ds(pl.multiple_of(me_d * block_y, 8), block_y)
-    t[me_d] = s[:, :, own_block, :]
-
-    for c in range(chunks):
-        for peer in peers_d:
-            deep_copy(c, peer, peer).wait_recv()
+    t[me_d] = s[me_d]
+
+    for c in range(len(chunks)):
+        for k in range(packs) if c == 0 else [packs + c - 1]:
+            for peer in peers_d:
+                deep_copy(k, peer, peer).wait_recv()
         spectrum = []
         for p in range(packs):
             parts = [
-                t[d, p, c * step:(c + 1) * step].reshape(step * block_y, LANES)
+                t[d, starts[c]:starts[c] + chunks[c], p].reshape(chunks[c] * block_y, LANES)
                 for d in range(deep)
             ]
             for f in range(pack):
@@ -166,8 +178,8 @@
                     + jnp.dot(high, tz[1], preferred_element_type=F32)
                     + jnp.dot(low, tz[0], preferred_element_type=F32)
                 )
-        for i in range(step):
-            x = c * step + i
+        for i in range(chunks[c]):
+            x = starts[c] + i
             weight = 1.0 / (1.0 + (base + sym_x[0, me_n * share_x + x]))
             rest = 1.0 - weight
             old = [value[i * block_y:(i + 1) * block_y] for value in spectrum]
@@ -177,7 +189,7 @@
                     total = total + coupling[f, g] * old[g]
                 out[f, x] = weight * old[f] + rest * total
 
-    for c in range(chunks):
+    for c in range(len(pieces)):
         for slot, peer in enumerate(peers_n):
             north_copy(c, peer, slot).wait_send()
         for peer in peers_d:
@@ -190,7 +202,8 @@
     size_y, size_z = share_y * north, share_z * deep
     share_x, block_y = size_x // north, size_y // deep
     packs = fields * share_z // LANES
-    chunks = min(CHUNKS, share_x)
+    unit = sum(SIZES)
+    chunks = [size * share_x // unit for size in SIZES] if share_x % unit == 0 else [share_x]
     high, low = basis_table(size_x)
     tx = jnp.asarray(np.concatenate([high, low, high], axis=1))
     high, low = basis_table(size_y)
@@ -215,15 +228,15 @@
             pltpu.VMEM(tx.shape, BF16),
             pltpu.VMEM(ty.shape, BF16),
             pltpu.VMEM(tz.shape, BF16),
-            pltpu.VMEM((packs, size_x, share_y, LANES), F32),
-            pltpu.VMEM((packs, share_x, size_y, LANES), F32),
-            pltpu.VMEM((packs, share_x, size_y, LANES), F32),
-            pltpu.VMEM((deep, packs, share_x, block_y, LANES), F32),
+            pltpu.VMEM((size_x, packs, share_y, LANES), F32),
+            pltpu.VMEM((north, share_x, packs, share_y, LANES), F32),
+            pltpu.VMEM((deep, share_x, packs, block_y, LANES), F32),
+            pltpu.VMEM((deep, share_x, packs, block_y, LANES), F32),
             pltpu.SemaphoreType.DMA((7 + packs,)),
-            pltpu.SemaphoreType.DMA((chunks, north - 1)),
-            pltpu.SemaphoreType.DMA((chunks, north - 1)),
-            pltpu.SemaphoreType.DMA((chunks, deep)),
-            pltpu.SemaphoreType.DMA((chunks, deep)),
+            pltpu.SemaphoreType.DMA((len(chunks) + packs - 1, north - 1)),
+            pltpu.SemaphoreType.DMA((len(chunks) + packs - 1, north - 1)),
+            pltpu.SemaphoreType.DMA((len(chunks) + packs - 1, deep)),
+            pltpu.SemaphoreType.DMA((len(chunks) + packs - 1, deep)),
         ],
         compiler_params=pltpu.CompilerParams(
             collective_id=0, has_side_effects=True, vmem_limit_bytes=need

time: 37.4 us -> 33.9 us (0.906)
  Pallas kernels: 35.7 us -> 32.5 us
    pallas_call x1, Pallas kernels: 35.7 us -> 32.5 us  [on_device(): pl.pallas_call(functools.partial(kernel, north, deep, chunks), out_shape=...]
where the time goes in v3:
time: 33.9 us; the launch traced here: 33.5 us
  Pallas kernels  32.5 us (96%)
  local copies, waits for them, and re-layouts  0.97 us (3%)
    pallas_call x1, Pallas kernels, on_device(): pl.pallas_call(functools.partial(kernel, north, deep, chunks), out_shape=...  32.5 us
    unnamed x1, local copies, waits for them, and re-layouts  0.97 us

profile of v3, /device:TPU:1, one launch (start us, length us, event | category | flops | bytes accessed | tf_op | source)
XLA Modules:
  0.0 33.5 jit_solution(865797421934970541)
XLA Ops:
  0.0 32.5 %shard_map.82 = f32[4,16,16,256]{3,2,1,0:T(8,128)S(1)} custom-call(f32[4,8,64,128]{3,2,1,0:T(8,128)} %bitcast.4, f32[4,4]{1,0:T(4,128)} %coupling_hbm.1, f32[1,128]{1,0:T(1,128)} %bitcast.6, f32[1,64]{1,0:T(1,128)} %bitcast.7, f32[1,256]{1,0:T(1,128)} %bitcast.5, bf16[128,384]{1,0:T(8,128)(2,1)} %constant.6.clone.tx_hbm, ...), custom_call_target="tpu_custom_call" | custom-call | tf_op jit(solution)/shard_map/pallas_call | solution.py:217
  32.5 1.0 %copy.10 = f32[4,16,16,256]{3,2,1,0:T(8,128)} copy(f32[4,16,16,256]{3,2,1,0:T(8,128)S(1)} %shard_map.82) | data formatting | bytes 2097152

commit v4 on v3

--- a/solution.py
+++ b/solution.py
@@ -48,9 +48,22 @@
     block_y = size_y // deep
     size_z = share_z * deep
     starts = [sum(chunks[:c]) for c in range(len(chunks))]
-    pieces = [(p, 1, starts[0], chunks[0]) for p in range(packs)]
-    pieces += [(0, packs, starts[c], chunks[c]) for c in range(1, len(chunks))]
+    pieces = []
+    for c in range(len(chunks)):
+        count = 1 if c in (0, len(chunks) - 1) else packs
+        pieces += [(p, count, starts[c], chunks[c]) for p in range(0, packs, count)]
     half = deep // 2
+
+    peers_n = [lax.rem(me_n + k, north) for k in range(1, north)]
+    side = me_d // half
+    peers_d = [(1 - side) * half + lax.rem(me_d + j, half) for j in range(half)]
+    peers_d += [side * half + lax.rem(me_d + j, half) for j in range(1, half)]
+
+    barrier = pltpu.get_barrier_semaphore()
+    for peer in peers_n:
+        pl.semaphore_signal(barrier, inc=1, device_id={"north": peer}, device_id_type=MESH)
+    for peer in peers_d:
+        pl.semaphore_signal(barrier, inc=1, device_id={"deep": peer}, device_id_type=MESH)
 
     loads = [pltpu.make_async_copy(tx_hbm, tx, load_sem.at[0])]
     for p in range(packs):
@@ -64,19 +77,8 @@
         pltpu.make_async_copy(source, target, load_sem.at[1 + packs + i])
         for i, (source, target) in enumerate(pairs)
     ]
-    for copy in loads + late:
+    for copy in loads:
         copy.start()
-
-    peers_n = [lax.rem(me_n + k, north) for k in range(1, north)]
-    side = me_d // half
-    peers_d = [(1 - side) * half + lax.rem(me_d + j, half) for j in range(half)]
-    peers_d += [side * half + lax.rem(me_d + j, half) for j in range(1, half)]
-
-    barrier = pltpu.get_barrier_semaphore()
-    for peer in peers_n:
-        pl.semaphore_signal(barrier, inc=1, device_id={"north": peer}, device_id_type=MESH)
-    for peer in peers_d:
-        pl.semaphore_signal(barrier, inc=1, device_id={"deep": peer}, device_id_type=MESH)
 
     def north_copy(c, peer, slot):
         p, count, x, size = pieces[c]
@@ -118,6 +120,8 @@
             pl.semaphore_wait(barrier, len(peers_n) + len(peers_d))
         for slot, peer in enumerate(peers_n):
             north_copy(p, peer, slot).start()
+    for copy in late:
+        copy.start()
 
     for c in range(packs, len(pieces)):
         for slot, peer in enumerate(peers_n):
@@ -159,11 +163,12 @@
     t[me_d] = s[me_d]
 
     for c in range(len(chunks)):
-        for k in range(packs) if c == 0 else [packs + c - 1]:
-            for peer in peers_d:
-                deep_copy(k, peer, peer).wait_recv()
         spectrum = []
         for p in range(packs):
+            for k, (first, _, start, _) in enumerate(pieces):
+                if start == starts[c] and first == p:
+                    for peer in peers_d:
+                        deep_copy(k, peer, peer).wait_recv()
             parts = [
                 t[d, starts[c]:starts[c] + chunks[c], p].reshape(chunks[c] * block_y, LANES)
                 for d in range(deep)
@@ -233,10 +238,10 @@
             pltpu.VMEM((deep, share_x, packs, block_y, LANES), F32),
             pltpu.VMEM((deep, share_x, packs, block_y, LANES), F32),
             pltpu.SemaphoreType.DMA((7 + packs,)),
-            pltpu.SemaphoreType.DMA((len(chunks) + packs - 1, north - 1)),
-            pltpu.SemaphoreType.DMA((len(chunks) + packs - 1, north - 1)),
-            pltpu.SemaphoreType.DMA((len(chunks) + packs - 1, deep)),
-            pltpu.SemaphoreType.DMA((len(chunks) + packs - 1, deep)),
+            pltpu.SemaphoreType.DMA((len(chunks) * packs, north - 1)),
+            pltpu.SemaphoreType.DMA((len(chunks) * packs, north - 1)),
+            pltpu.SemaphoreType.DMA((len(chunks) * packs, deep)),
+            pltpu.SemaphoreType.DMA((len(chunks) * packs, deep)),
         ],
         compiler_params=pltpu.CompilerParams(
             collective_id=0, has_side_effects=True, vmem_limit_bytes=need

time: 33.9 us -> 35.3 us (1.041)
  Pallas kernels: 32.5 us -> 34.2 us
    pallas_call x1, Pallas kernels: 32.5 us -> 34.2 us  [on_device(): pl.pallas_call(functools.partial(kernel, north, deep, chunks), out_shape=...]
where the time goes in v4:
time: 35.3 us; the launch traced here: 35.2 us
  Pallas kernels  34.2 us (97%)
  local copies, waits for them, and re-layouts  0.97 us (3%)
    pallas_call x1, Pallas kernels, on_device(): pl.pallas_call(functools.partial(kernel, north, deep, chunks), out_shape=...  34.2 us
    unnamed x1, local copies, waits for them, and re-layouts  0.97 us

profile of v4, /device:TPU:1, one launch (start us, length us, event | category | flops | bytes accessed | tf_op | source)
XLA Modules:
  0.0 35.2 jit_solution(3986758274285580958)
XLA Ops:
  0.0 34.2 %shard_map.82 = f32[4,16,16,256]{3,2,1,0:T(8,128)S(1)} custom-call(f32[4,8,64,128]{3,2,1,0:T(8,128)} %bitcast.4, f32[4,4]{1,0:T(4,128)} %coupling_hbm.1, f32[1,128]{1,0:T(1,128)} %bitcast.6, f32[1,64]{1,0:T(1,128)} %bitcast.7, f32[1,256]{1,0:T(1,128)} %bitcast.5, bf16[128,384]{1,0:T(8,128)(2,1)} %constant.6.clone.tx_hbm, ...), custom_call_target="tpu_custom_call" | custom-call | tf_op jit(solution)/shard_map/pallas_call | solution.py:222
  34.2 1.0 %copy.10 = f32[4,16,16,256]{3,2,1,0:T(8,128)} copy(f32[4,16,16,256]{3,2,1,0:T(8,128)S(1)} %shard_map.82) | data formatting | bytes 2097152
